TPU v7x, 32 devices: a whole 2x2x4 slice. The times are simulated.
32 devices in a mesh: groups: 2 (over x), prompt: 8 (over z, y), resp: 2 (over core).
Axes of the slice: x: 2, y: 2, z: 4, core: 2. Of those that a mesh axis runs over, the one named last changes fastest.
Arguments:
- queries: bfloat16 [16, 512, 1024], P(('groups', 'prompt'), 'resp'), parts along dimension 0, may hold values from -4096 to 4096
- grad_out: bfloat16 [16, 512, 1024], P(('groups', 'prompt'), 'resp'), parts along dimension 0, may hold values from -48 to 48
- keys_resp: bfloat16 [16, 512, 128], P(('groups', 'prompt'), 'resp'), parts along dimension 0, may hold values from -6 to 6
- values_resp: bfloat16 [16, 512, 128], P(('groups', 'prompt'), 'resp'), parts along dimension 0, may hold values from -6 to 6
- keys_prefix: bfloat16 [1024, 128], P(('groups', 'prompt')), parts along dimension 0, may hold values from -32 to 32
- values_prefix: bfloat16 [1024, 128], P(('groups', 'prompt')), parts along dimension 0, may hold values from -6 to 6
- lengths: int32 [16], P(('groups', 'prompt')), parts along dimension 0, may hold values from 1 to 512, as said below
- block_plan: int32 [16, 4], P(('groups', 'prompt'), 'resp'), parts along dimension 0, may hold values from 0 to 3, as said below
Outputs:
- query_grads: float32 [16, 512, 1024], P(('groups', 'prompt'), 'resp'), parts along dimension 0
- prefix_keygrad: float32 [1024, 128], P(('groups', 'prompt', 'resp')), parts along dimension 0
- prefix_valgrad: float32 [1024, 128], P(('groups', 'prompt', 'resp')), parts along dimension 0
- reply_keygrad: float32 [16, 512, 128], P(('groups', 'prompt'), 'resp'), parts along dimension 0
- reply_valgrad: float32 [16, 512, 128], P(('groups', 'prompt'), 'resp'), parts along dimension 0
There are 2 independent parts, one for each index of `groups`. A program takes and returns all parts, laid end to end along the dimension named above; each array names one. Nothing has to cross between parts.
Inputs may be any that keep to these rules, and one draw needn't show every extreme that they name: `lengths`: one response has exactly 512 live positions. `block_plan`: each row is a permutation of 0 to 3; for every m, blocks 2 * m and 2 * m + 1 stand in different halves of the row.
All inputs are finite; a program needn't handle non-finite values.
Results may differ from a plain program's by a relative error of at most 0.0029.
Values may be sent and summed in bfloat16 or wider, within the bound.
No kernel may reach another device: no remote copies, remote signals or barrier semaphores. Data moves between devices by JAX's collectives and lax.ppermute only.
A program may use at most 64 MiB of HBM per device.

v0:
```python
import jax
import jax.numpy as jnp
from jax import lax
from jax.sharding import PartitionSpec as P

RBLK = 128


def block_terms(
    query_block, grad_block, first_row, length, all_keys, all_values, prefix_len, head_count
):
    row_count = query_block.shape[0]
    head_width = all_keys.shape[1]
    key_count = all_keys.shape[0]
    score_scale = head_width ** (-0.5)
    positions = first_row + jnp.arange(row_count, dtype=jnp.int32)
    key_index = jnp.arange(key_count, dtype=jnp.int32)
    relative = key_index - prefix_len
    visible = (key_index[None, :] < prefix_len) | (relative[None, :] <= positions[:, None]) & (
        relative[None, :] < length
    )
    live_rows = positions < length
    query_heads = query_block.reshape(row_count, head_count, head_width)
    grad_heads = jnp.where(
        live_rows[:, None, None],
        grad_block.reshape(row_count, head_count, head_width),
        jnp.zeros((), jnp.bfloat16),
    )
    half_heads = head_count // 2

    def active_block(unused):
        grad_parts = []
        grad_k = jnp.zeros((key_count, head_width), jnp.float32)
        grad_v = jnp.zeros((key_count, head_width), jnp.float32)
        for group_index in range(2):
            query_part = query_heads[:, group_index * half_heads : (group_index + 1) * half_heads]
            grad_part = grad_heads[:, group_index * half_heads : (group_index + 1) * half_heads]
            scores = (
                jnp.einsum("rhd,kd->rhk", query_part, all_keys, preferred_element_type=jnp.float32)
                * score_scale
            )
            scores = jnp.where(visible[:, None, :], scores, -jnp.inf)
            row_max = jnp.max(scores, -1, keepdims=True)
            exponent = jnp.exp(scores - row_max)
            weights = exponent / jnp.sum(exponent, -1, keepdims=True)
            grad_weight = jnp.einsum(
                "rhd,kd->rhk", grad_part, all_values, preferred_element_type=jnp.float32
            )
            row_inner = jnp.sum(weights * grad_weight, -1, keepdims=True)
            grad_score = (weights * (grad_weight - row_inner)).astype(jnp.bfloat16)
            rounded_weights = weights.astype(jnp.bfloat16)
            grad_query = (
                jnp.einsum("rhk,kd->rhd", grad_score, all_keys, preferred_element_type=jnp.float32)
                * score_scale
            )
            grad_parts.append(grad_query)
            grad_k = (
                grad_k
                + jnp.einsum(
                    "rhk,rhd->kd", grad_score, query_part, preferred_element_type=jnp.float32
                )
                * score_scale
            )
            grad_v = grad_v + jnp.einsum(
                "rhk,rhd->kd", rounded_weights, grad_part, preferred_element_type=jnp.float32
            )
        joined = jnp.concatenate(grad_parts, 1).reshape(row_count, head_count * head_width)
        return (joined, grad_k, grad_v)

    def empty_block(unused):
        return (
            jnp.zeros((row_count, head_count * head_width), jnp.float32),
            jnp.zeros((key_count, head_width), jnp.float32),
            jnp.zeros((key_count, head_width), jnp.float32),
        )

    return lax.cond(first_row < length, active_block, empty_block, 0)


def local(
    queries, grad_out, keys_resp, values_resp, keys_prefix, values_prefix, lengths, block_plan
):
    core_count = lax.axis_size("resp")
    slot_count = queries.shape[1]
    head_width = keys_prefix.shape[1]
    full_width = queries.shape[2]
    head_count = full_width // head_width
    block_count = slot_count // RBLK
    total_blocks = block_count * core_count
    length = lengths[0]
    prefix_keys, prefix_values = (
        lax.all_gather(keys_prefix, "prompt", axis=0, tiled=True),
        lax.all_gather(values_prefix, "prompt", axis=0, tiled=True),
    )
    prefix_len = prefix_keys.shape[0]
    plan_row = block_plan[0]
    query_all, grad_all, reply_keys, reply_values = (
        lax.all_gather(queries, "resp", axis=1, tiled=True),
        lax.all_gather(grad_out, "resp", axis=1, tiled=True),
        lax.all_gather(keys_resp, "resp", axis=1, tiled=True),
        lax.all_gather(values_resp, "resp", axis=1, tiled=True),
    )
    query_work = jnp.take(query_all.reshape(total_blocks, RBLK, full_width), plan_row, axis=0)
    grad_work = jnp.take(grad_all.reshape(total_blocks, RBLK, full_width), plan_row, axis=0)
    starts = plan_row * RBLK
    all_keys = jnp.concatenate([prefix_keys, reply_keys[0]], 0)
    all_values = jnp.concatenate([prefix_values, reply_values[0]], 0)

    def advance(totals, block_item):
        query_block, grad_block, first_row = block_item
        grad_query, grad_k, grad_v = block_terms(
            query_block, grad_block, first_row, length, all_keys, all_values, prefix_len, head_count
        )
        return ((totals[0] + grad_k, totals[1] + grad_v), grad_query)

    zeros = jnp.zeros(all_keys.shape, jnp.float32)
    totals, grad_blocks = lax.scan(advance, (zeros, zeros), (query_work, grad_work, starts))
    local_grads = grad_blocks.reshape(1, slot_count, full_width)
    key_total, value_total = totals
    reply_keygrad, reply_valgrad = (
        lax.psum_scatter(key_total[prefix_len:][None], "resp", scatter_dimension=1, tiled=True),
        lax.psum_scatter(value_total[prefix_len:][None], "resp", scatter_dimension=1, tiled=True),
    )
    prefix_k = key_total[:prefix_len]
    prefix_v = value_total[:prefix_len]
    prefix_keygrad, prefix_valgrad = (
        lax.psum_scatter(prefix_k, ("prompt", "resp"), scatter_dimension=0, tiled=True),
        lax.psum_scatter(prefix_v, ("prompt", "resp"), scatter_dimension=0, tiled=True),
    )
    return (local_grads, prefix_keygrad, prefix_valgrad, reply_keygrad, reply_valgrad)


def solution(mesh):
    placed = (
        P(("groups", "prompt"), "resp", None),
        P(("groups", "prompt"), "resp", None),
        P(("groups", "prompt"), "resp", None),
        P(("groups", "prompt"), "resp", None),
        P(("groups", "prompt"), None),
        P(("groups", "prompt"), None),
        P(("groups", "prompt")),
        P(("groups", "prompt"), "resp"),
    )
    return jax.shard_map(
        local,
        mesh=mesh,
        in_specs=placed,
        out_specs=(
            P(("groups", "prompt"), "resp", None),
            P(("groups", "prompt", "resp"), None),
            P(("groups", "prompt", "resp"), None),
            P(("groups", "prompt"), "resp", None),
            P(("groups", "prompt"), "resp", None),
        ),
        check_vma=False,
    )
```

profile of v0, /device:TPU:0, one launch (start us, length us, event | category | flops | bytes accessed | tf_op | source)
XLA Modules:
  0.0 276.5 jit_solution(17285941282429215589)
XLA Ops:
  7.2 0.0 copy-start.1
  7.2 0.0 copy-start.2
  7.2 0.0 copy-start.5
  7.2 0.0 all-gather.5.cloned.1.call-start
  7.2 0.7 all-gather.5.cloned.1.call-update
  7.9 0.0 all-gather.3.cloned.1.call-start
  8.0 0.7 all-gather.3.cloned.1.call-update
  8.7 0.0 reduce-scatter.5.cloned.1.call-start
  8.8 2.2 all_gather.20
  11.0 32.4 %all_gather.19 = bf16[512,128]{1,0:T(8,128)(2,1)S(1)} all-gather(bf16[64,128]{1,0:T(8,128)(2,1)} %param.18), channel_id=1, replica_groups=mesh['groups'=2,'prompt'=8,'resp'=2] {'prompt'}, dimensions={0}, use_global_device_ids=true | all-gather | bytes 147456 | tf_op jit(solution)/shard_map/all_gather | solution.py:92
  43.4 0.1 copy.58
  43.6 0.0 copy-done.1
  43.6 1.9 all_gather.23
  45.5 0.0 copy-done.2
  45.5 30.5 %all_gather.22 = bf16[512,128]{1,0:T(8,128)(2,1)S(1)} all-gather(bf16[64,128]{1,0:T(8,128)(2,1)S(1)} %copy-done.2), channel_id=1, replica_groups=mesh['groups'=2,'prompt'=8,'resp'=2] {'prompt'}, dimensions={0}, use_global_device_ids=true | all-gather | bytes 147456 | tf_op jit(solution)/shard_map/all_gather | solution.py:93
  76.0 0.0 copy-done.5
  76.0 0.7 pad_maximum_fusion.2
  76.8 0.0 all-gather.5.cloned.1.call-done
  76.8 1.8 gather_fusion.1
  78.6 0.0 all-gather.3.cloned.1.call-done
  78.6 1.8 gather_fusion
  80.4 0.2 broadcast_select_fusion.1
  80.6 1.0 copy.59
  81.6 1.0 copy.57
  82.6 14.9 %while.17 = (s32[]{:T(128)}, f32[1024,128]{1,0:T(8,128)}, f32[1024,128]{1,0:T(8,128)}, f32[2,128,1024]{2,1,0:T(8,128)}, s32[2]{0:T(128)S(1)}, /*index=5*/s32[]{:...) while((s32[]{:T(128)}, f32[1024,128]{1,0:T(8,128)}, ...), condition=%wide.region_9.11_spmd.clone, body=%wide.region_0.10_spmd.clone.sunk | while | flops 1629102464 | bytes 53665412 | solution.py:117
  82.6 0.6 dynamic_slice.32
  84.5 1.8 conditional.3
  84.5 0.8 broadcast.91.clone
  85.4 0.9 broadcast.91
  86.3 0.0 copy-start.3
  86.3 2.4 select_add_fusion.3
  88.7 0.2 copy.74
  88.9 0.0 copy-done.3
  88.9 0.0 copy-start.4
  88.9 1.0 copy-done.4
  89.9 0.6 dynamic_slice.32
  91.8 1.8 conditional.3
  91.8 0.8 broadcast.91.clone
  92.7 0.9 broadcast.91
  93.6 0.0 copy-start.3
  93.6 2.7 select_add_fusion.3
  96.3 0.2 copy.74
  96.5 0.0 copy-done.3
  96.5 0.0 copy-start.4
  96.6 1.0 copy-done.4
  97.5 1.9 slice_bitcast_fusion.1
  99.4 0.0 reduce-scatter.5.cloned.1.call-update
  99.4 0.0 reduce-scatter.7.cloned.1.call-start
  99.4 1.9 slice_bitcast_fusion
  101.3 0.0 reduce-scatter.7.cloned.1.call-update
  101.3 0.0 reduce-scatter.9.cloned.1.call-start
  101.4 0.5 reduce-scatter.9.cloned.1.call-update
  101.9 0.0 reduce-scatter.11.cloned.1.call-start
  102.0 0.5 reduce-scatter.11.cloned.1.call-update
  102.5 87.4 %reduce-scatter.5.cloned.1.call-done = f32[32,128]{1,0:T(8,128)} async-done(((f32[512,128]{1,0:T(8,128)}), f32[32,128]{1,0:T(8,128)}) %reduce-scatter.5.cloned.1.call-update) | async-done | bytes 16400 | tf_op jit(solution)/shard_map/reduce_scatter | solution.py:127
  189.9 58.7 %reduce-scatter.7.cloned.1.call-done = f32[32,128]{1,0:T(8,128)} async-done(((f32[512,128]{1,0:T(8,128)}), f32[32,128]{1,0:T(8,128)}) %reduce-scatter.7.cloned.1.call-update) | async-done | bytes 16400 | tf_op jit(solution)/shard_map/reduce_scatter | solution.py:128
  248.7 9.4 %reduce-scatter.9.cloned.1.call-done = f32[1,256,128]{2,1,0:T(8,128)} async-done(((f32[1,512,128]{2,1,0:T(8,128)}), f32[1,256,128]{2,1,0:T(8,128)}) %reduce-scatter.9.cloned.1.call-update) | async-done | bytes 131088 | tf_op jit(solution)/shard_map/reduce_scatter | solution.py:121
  258.1 11.5 %reduce-scatter.11.cloned.1.call-done = f32[1,256,128]{2,1,0:T(8,128)} async-done(((f32[1,512,128]{2,1,0:T(8,128)}), f32[1,256,128]{2,1,0:T(8,128)}) %reduce-scatter.11.cloned.1.call-update) | async-done | bytes 131088 | tf_op jit(solution)/shard_map/reduce_scatter | solution.py:122
  (17 shorter events, 0.2 us)
Async XLA Ops:
  7.2 36.4 %copy-start.1 = (bf16[1,256,128]{2,1,0:T(8,128)(2,1)S(1)}, bf16[1,256,128]{2,1,0:T(8,128)(2,1)}, u32[]{:S(2)}) copy-start(bf16[1,256,128]{2,1,0:T(8,128)(2,1)} %param.17) | copy-start | bytes 196612
  7.2 38.3 %copy-start.2 = (bf16[64,128]{1,0:T(8,128)(2,1)S(1)}, bf16[64,128]{1,0:T(8,128)(2,1)}, u32[]{:S(2)}) copy-start(bf16[64,128]{1,0:T(8,128)(2,1)} %param.19) | copy-start | bytes 49156
  7.2 68.8 %copy-start.5 = (s32[1,2]{1,0:T(1,128)S(1)}, s32[1,2]{1,0:T(1,128)}, u32[]{:S(2)}) copy-start(s32[1,2]{1,0:T(1,128)} %param.21) | copy-start | bytes 28
  7.2 69.6 %all-gather.5.cloned.1.call-start = ((), (), s32[]{:S(2)}) async-start(), calls=%async_computation.5 | async-start | bytes 1572864 | tf_op jit(solution)/shard_map/all_gather | solution.py:99
  7.9 70.7 %all-gather.3.cloned.1.call-start = ((), (), s32[]{:S(2)}) async-start(), calls=%async_computation.4 | async-start | bytes 1572864 | tf_op jit(solution)/shard_map/all_gather | solution.py:98
  8.7 181.2 %reduce-scatter.5.cloned.1.call-start = ((), (), s32[]{:S(2)}) async-start(), calls=%async_computation.6 | async-start | bytes 278528 | tf_op jit(solution)/shard_map/reduce_scatter | solution.py:127
  86.3 2.6 copy-start.3
  88.9 1.0 copy-start.4
  93.6 2.9 %copy-start.3 = (f32[2,128,1024]{2,1,0:T(8,128)S(1)}, f32[2,128,1024]{2,1,0:T(8,128)}, u32[]{:S(2)}) copy-start(f32[2,128,1024]{2,1,0:T(8,128)} %get-tuple-element.493) | copy-start | bytes 3145732 | tf_op jit(solution)/shard_map/while
  96.5 1.0 copy-start.4
  99.4 149.3 %reduce-scatter.7.cloned.1.call-start = ((), (), s32[]{:S(2)}) async-start(), calls=%async_computation.7 | async-start | bytes 278528 | tf_op jit(solution)/shard_map/reduce_scatter | solution.py:128
  101.3 156.7 %reduce-scatter.9.cloned.1.call-start = ((), (), s32[]{:S(2)}) async-start(), calls=%async_computation.8 | async-start | bytes 393216 | tf_op jit(solution)/shard_map/reduce_scatter | solution.py:121
  101.9 167.7 %reduce-scatter.11.cloned.1.call-start = ((), (), s32[]{:S(2)}) async-start(), calls=%async_computation.9 | async-start | bytes 393216 | tf_op jit(solution)/shard_map/reduce_scatter | solution.py:122
Sparse Core Ops, SparseCore 0:
  9.5 11.7 all-gather.4
  22.9 10.1 all-gather.2
  99.5 90.3 reduce-scatter.4
  193.9 54.7 reduce-scatter.6
  251.3 6.7 reduce-scatter.8
  260.7 8.8 reduce-scatter.10
where the time goes:
time: 277 us; the launch traced here: 276 us
  waiting for transfers between devices  170 us (61%)
  blocking collectives  67.1 us (24%)
  local copies, waits for them, and re-layouts  16.6 us (6%)
  between operations  14.2 us (5%)
  other arithmetic  6.03 us (2%)
    reduce_scatter x1, waiting for transfers between devices, local(): lax.psum_scatter(prefix_k, ('prompt', 'resp'), scatter_dimension=0, tiled...  87.4 us
    reduce_scatter x1, waiting for transfers between devices, local(): lax.psum_scatter(prefix_v, ('prompt', 'resp'), scatter_dimension=0, tiled...  58.7 us
    all_gather x1, blocking collectives, local(): lax.all_gather(keys_prefix, 'prompt', axis=0, tiled=True)  32.4 us
    all_gather x1, blocking collectives, local(): lax.all_gather(values_prefix, 'prompt', axis=0, tiled=True)  30.5 us
    reduce_scatter x1, waiting for transfers between devices, local(): lax.psum_scatter(value_total[prefix_len:][None], 'resp', scatter_dimensio...  11.5 us
    reduce_scatter x1, waiting for transfers between devices, local(): lax.psum_scatter(key_total[prefix_len:][None], 'resp', scatter_dimension=...  9.41 us
  transfers between devices with their start and end apart: 6, of which 4 were waited for; matrix products, arithmetic and copies ran while one was open for 2% of the time, Pallas kernels for 0%

commit v1 on v0

--- a/solution.py
+++ b/solution.py
@@ -89,7 +89,10 @@
     total_blocks = block_count * core_count
     length = lengths[0]
     prefix_keys, prefix_values = (
-        lax.all_gather(keys_prefix, "prompt", axis=0, tiled=True),
+        jnp.concatenate(
+            lax.all_to_all(jnp.stack([keys_prefix] * lax.axis_size("prompt")), "prompt", 0, 0),
+            axis=0,
+        ),
         lax.all_gather(values_prefix, "prompt", axis=0, tiled=True),
     )
     prefix_len = prefix_keys.shape[0]

time: 277 us -> 255 us (0.921)
  blocking collectives: 67.1 us -> 35.2 us
  starting transfers between devices: 0.23 us -> 7.54 us
    all_gather x1 -> x0, blocking collectives: 32.4 us -> none  [local(): lax.all_gather(keys_prefix, 'prompt', axis=0, tiled=True)]
    all_to_all x0 -> x1, starting transfers between devices: none -> 7.31 us  [local(): lax.all_to_all(jnp.stack([keys_prefix] * lax.axis_size('prompt')), 'promp...]
  transfers between devices with their start and end apart: 6 -> 7, of which waited for: 4 -> 4; matrix products, arithmetic and copies ran while one was open for 2% -> 3% of each run, Pallas kernels for 0% -> 0%
where the time goes in v1:
time: 255 us; the launch traced here: 254 us
  waiting for transfers between devices  169 us (66%)
  blocking collectives  35.2 us (14%)
  local copies, waits for them, and re-layouts  18 us (7%)
  between operations  14.2 us (6%)
  starting transfers between devices  7.54 us (3%)
  other arithmetic  6.68 us (3%)
  loops' own time  2.75 us (1%)
    reduce_scatter x1, waiting for transfers between devices, local(): lax.psum_scatter(prefix_k, ('prompt', 'resp'), scatter_dimension=0, tiled...  87.2 us
    reduce_scatter x1, waiting for transfers between devices, local(): lax.psum_scatter(prefix_v, ('prompt', 'resp'), scatter_dimension=0, tiled...  58.7 us
    all_gather x1, blocking collectives, local(): lax.all_gather(values_prefix, 'prompt', axis=0, tiled=True)  31.2 us
    reduce_scatter x1, waiting for transfers between devices, local(): lax.psum_scatter(value_total[prefix_len:][None], 'resp', scatter_dimensio...  11.5 us
    reduce_scatter x1, waiting for transfers between devices, local(): lax.psum_scatter(key_total[prefix_len:][None], 'resp', scatter_dimension=...  9.47 us
    all_to_all x1, starting transfers between devices, local(): lax.all_to_all(jnp.stack([keys_prefix] * lax.axis_size('prompt')), 'promp...  7.31 us
  transfers between devices with their start and end apart: 7, of which 4 were waited for; matrix products, arithmetic and copies ran while one was open for 3% of the time, Pallas kernels for 0%

profile of v1, /device:TPU:0, one launch (start us, length us, event | category | flops | bytes accessed | tf_op | source)
XLA Modules:
  0.0 253.9 jit_solution(14914734943026473867)
XLA Ops:
  7.2 0.0 copy-start.4
  7.2 0.0 copy-start.1
  7.2 0.0 all-gather.5.cloned.1.call-start
  7.2 0.7 all-gather.5.cloned.1.call-update
  7.9 0.0 all-gather.3.cloned.1.call-start
  8.0 0.7 all-gather.3.cloned.1.call-update
  8.7 1.4 stack.2
  10.1 7.3 %all-to-all-start = ((bf16[8,64,128]{2,1,0:T(8,128)(2,1)}), bf16[8,64,128]{2,1,0:T(8,128)(2,1)S(1)}, u32[]{:S(2)}, u32[]{:S(2)}) async-start(bf16[8,64,128]{2,1,0:T(8,128)(2,1)} %stack.2), calls=%async_computation | async-start | bytes 262144 | tf_op jit(solution)/shard_map/all_to_all | solution.py:93
  17.4 0.0 reduce-scatter.5.cloned.1.call-start
  17.4 2.1 all_gather.19
  19.5 31.2 %all_gather.18 = bf16[512,128]{1,0:T(8,128)(2,1)S(1)} all-gather(bf16[64,128]{1,0:T(8,128)(2,1)} %param.19), channel_id=1, replica_groups=mesh['groups'=2,'prompt'=8,'resp'=2] {'prompt'}, dimensions={0}, use_global_device_ids=true | all-gather | bytes 147456 | tf_op jit(solution)/shard_map/all_gather | solution.py:96
  50.8 0.7 compare_select_fusion
  51.4 0.7 pad_maximum_fusion.2
  52.2 0.0 copy-done.1
  52.2 1.9 all_gather.16
  54.1 0.0 copy-done.4
  54.1 0.0 all-to-all-done
  54.1 0.1 copy.43
  54.3 0.0 all-gather.5.cloned.1.call-done
  54.3 1.8 gather_fusion.1
  56.1 0.0 all-gather.3.cloned.1.call-done
  56.1 1.8 gather_fusion
  57.9 0.2 broadcast_select_fusion.1
  58.1 1.0 copy.44
  59.1 1.0 copy.42
  60.1 14.9 %while.17 = (s32[]{:T(128)}, f32[1024,128]{1,0:T(8,128)}, f32[1024,128]{1,0:T(8,128)}, f32[2,128,1024]{2,1,0:T(8,128)}, s32[2]{0:T(128)S(1)}, /*index=5*/s32[]{:...) while((s32[]{:T(128)}, f32[1024,128]{1,0:T(8,128)}, ...), condition=%wide.region_9.11_spmd.clone, body=%wide.region_0.10_spmd.clone.sunk | while | flops 1629102464 | bytes 53665412 | solution.py:120
  60.1 0.6 dynamic_slice.32
  62.0 1.8 conditional.3
  62.0 0.8 broadcast.93.clone
  62.9 0.9 broadcast.93
  63.8 0.0 copy-start.2
  63.8 2.4 select_add_fusion.3
  66.2 0.2 copy.59
  66.4 0.0 copy-done.2
  66.4 0.0 copy-start.3
  66.5 1.0 copy-done.3
  67.4 0.6 dynamic_slice.32
  69.3 1.8 conditional.3
  69.4 0.8 broadcast.93.clone
  70.2 0.9 broadcast.93
  71.1 0.0 copy-start.2
  71.1 2.7 %select_add_fusion.3 = (f32[1024,128]{1,0:T(8,128)}, f32[1024,128]{1,0:T(8,128)}) fusion(f32[1024,128]{1,0:T(8,128)} %get-tuple-element.467, f32[1024,128]{1,0:T(8,128)} %get-tuple-element.492, pred[]{:T(512)S(6)} %compare.3, f32[1024,128]{1,0:T(8,128)} %get-tuple-element.468, f32[1024,128]{1,0:T(8,128)} %get-tuple-element.491), kind=kLoop, calls=%fused_computation.61.clone.1 | loop fusion | flops 524288 | bytes 3145729 | tf_op jit(solution)/shard_map/while/body/eval_jaxpr/add | solution.py:117
  73.8 0.2 copy.59
  74.0 0.0 copy-done.2
  74.1 0.0 copy-start.3
  74.1 1.0 copy-done.3
  75.0 1.9 slice_bitcast_fusion.1
  76.9 0.0 reduce-scatter.5.cloned.1.call-update
  76.9 0.0 reduce-scatter.7.cloned.1.call-start
  77.0 1.9 slice_bitcast_fusion
  78.8 0.0 reduce-scatter.7.cloned.1.call-update
  78.9 0.0 reduce-scatter.9.cloned.1.call-start
  78.9 0.5 reduce-scatter.9.cloned.1.call-update
  79.5 0.0 reduce-scatter.11.cloned.1.call-start
  79.5 0.5 reduce-scatter.11.cloned.1.call-update
  80.0 87.2 %reduce-scatter.5.cloned.1.call-done = f32[32,128]{1,0:T(8,128)} async-done(((f32[512,128]{1,0:T(8,128)}), f32[32,128]{1,0:T(8,128)}) %reduce-scatter.5.cloned.1.call-update) | async-done | bytes 16400 | tf_op jit(solution)/shard_map/reduce_scatter | solution.py:130
  167.3 58.7 %reduce-scatter.7.cloned.1.call-done = f32[32,128]{1,0:T(8,128)} async-done(((f32[512,128]{1,0:T(8,128)}), f32[32,128]{1,0:T(8,128)}) %reduce-scatter.7.cloned.1.call-update) | async-done | bytes 16400 | tf_op jit(solution)/shard_map/reduce_scatter | solution.py:131
  226.0 9.5 %reduce-scatter.9.cloned.1.call-done = f32[1,256,128]{2,1,0:T(8,128)} async-done(((f32[1,512,128]{2,1,0:T(8,128)}), f32[1,256,128]{2,1,0:T(8,128)}) %reduce-scatter.9.cloned.1.call-update) | async-done | bytes 131088 | tf_op jit(solution)/shard_map/reduce_scatter | solution.py:124
  235.5 11.5 %reduce-scatter.11.cloned.1.call-done = f32[1,256,128]{2,1,0:T(8,128)} async-done(((f32[1,512,128]{2,1,0:T(8,128)}), f32[1,256,128]{2,1,0:T(8,128)}) %reduce-scatter.11.cloned.1.call-update) | async-done | bytes 131088 | tf_op jit(solution)/shard_map/reduce_scatter | solution.py:125
  (16 shorter events, 0.2 us)
Async XLA Ops:
  7.2 46.9 %copy-start.4 = (s32[1,2]{1,0:T(1,128)S(1)}, s32[1,2]{1,0:T(1,128)}, u32[]{:S(2)}) copy-start(s32[1,2]{1,0:T(1,128)} %param.21) | copy-start | bytes 28
  7.2 45.0 %copy-start.1 = (bf16[1,256,128]{2,1,0:T(8,128)(2,1)S(1)}, bf16[1,256,128]{2,1,0:T(8,128)(2,1)}, u32[]{:S(2)}) copy-start(bf16[1,256,128]{2,1,0:T(8,128)(2,1)} %param.16) | copy-start | bytes 196612
  7.2 47.1 %all-gather.5.cloned.1.call-start = ((), (), s32[]{:S(2)}) async-start(), calls=%async_computation.6 | async-start | bytes 1572864 | tf_op jit(solution)/shard_map/all_gather | solution.py:102
  7.9 48.2 %all-gather.3.cloned.1.call-start = ((), (), s32[]{:S(2)}) async-start(), calls=%async_computation.5 | async-start | bytes 1572864 | tf_op jit(solution)/shard_map/all_gather | solution.py:101
  10.1 44.0 %all-to-all-start = ((bf16[8,64,128]{2,1,0:T(8,128)(2,1)}), bf16[8,64,128]{2,1,0:T(8,128)(2,1)S(1)}, u32[]{:S(2)}, u32[]{:S(2)}) async-start(bf16[8,64,128]{2,1,0:T(8,128)(2,1)} %stack.2), calls=%async_computation | async-start | bytes 262144 | tf_op jit(solution)/shard_map/all_to_all | solution.py:93
  17.4 149.9 %reduce-scatter.5.cloned.1.call-start = ((), (), s32[]{:S(2)}) async-start(), calls=%async_computation.7 | async-start | bytes 278528 | tf_op jit(solution)/shard_map/reduce_scatter | solution.py:130
  63.8 2.6 %copy-start.2 = (f32[2,128,1024]{2,1,0:T(8,128)S(1)}, f32[2,128,1024]{2,1,0:T(8,128)}, u32[]{:S(2)}) copy-start(f32[2,128,1024]{2,1,0:T(8,128)} %get-tuple-element.493) | copy-start | bytes 3145732 | tf_op jit(solution)/shard_map/while
  66.4 1.0 copy-start.3
  71.1 2.9 %copy-start.2 = (f32[2,128,1024]{2,1,0:T(8,128)S(1)}, f32[2,128,1024]{2,1,0:T(8,128)}, u32[]{:S(2)}) copy-start(f32[2,128,1024]{2,1,0:T(8,128)} %get-tuple-element.493) | copy-start | bytes 3145732 | tf_op jit(solution)/shard_map/while
  74.1 1.0 copy-start.3
  76.9 149.1 %reduce-scatter.7.cloned.1.call-start = ((), (), s32[]{:S(2)}) async-start(), calls=%async_computation.8 | async-start | bytes 278528 | tf_op jit(solution)/shard_map/reduce_scatter | solution.py:131
  78.9 156.6 %reduce-scatter.9.cloned.1.call-start = ((), (), s32[]{:S(2)}) async-start(), calls=%async_computation.9 | async-start | bytes 393216 | tf_op jit(solution)/shard_map/reduce_scatter | solution.py:124
  79.5 167.6 %reduce-scatter.11.cloned.1.call-start = ((), (), s32[]{:S(2)}) async-start(), calls=%async_computation.10 | async-start | bytes 393216 | tf_op jit(solution)/shard_map/reduce_scatter | solution.py:125
Sparse Core Ops, SparseCore 0:
  9.5 11.7 all-gather.4
  22.9 10.1 all-gather.2
  77.0 90.1 reduce-scatter.4
  171.2 54.7 reduce-scatter.6
  228.6 6.7 reduce-scatter.8
  238.1 8.8 reduce-scatter.10
